TPU v7x, 32 devices: a whole 2x2x4 slice. The times are simulated.
32 devices in a mesh: grp: 2 (over y), slab: 4 (over z), ang: 4 (over x, core).
Axes of the slice: x: 2, y: 2, z: 4, core: 2. Of those that a mesh axis runs over, the one named last changes fastest.
Arguments:
- volume: bfloat16 [16, 256, 1024], P(('grp', 'slab')), parts along dimension 0, may hold values from -6 to 6
- ray_weights: bfloat16 [8, 1024, 1024], P('ang'), may hold values from -0.0625 to 0.0625
- row_offsets: int32 [8, 8], P('ang'), may hold values from 0 to 8
- measured: float32 [16, 256, 1024], P(('grp', 'ang'), 'slab'), parts along dimension 0, may hold values from -6 to 6
- shifts: float32 [16], P(('grp', 'ang')), parts along dimension 0, may hold values from -4 to 4
Outputs:
- updated_volume: bfloat16 [16, 256, 1024], P(('grp', 'slab')), parts along dimension 0
- last_residual: float32 [16, 256, 1024], P(('grp', 'ang'), 'slab'), parts along dimension 0
- shift_slope: float32 [16], P(('grp', 'ang')), parts along dimension 0
There are 2 independent parts, one for each index of `grp`. A program takes and returns all parts, laid end to end along the dimension named above; an argument that names none is the same for every part. Nothing has to cross between parts.
All inputs are finite; a program needn't handle non-finite values.
Results may differ from a plain program's by a relative error of at most 0.006.
Values may be sent and summed in bfloat16 or wider, within the bound.
A program may use at most 128 MiB of HBM per device.

v0:
```python
import math
import jax
import jax.numpy as jnp
from jax import lax
from jax.sharding import PartitionSpec as P

Y = 256
X = 1024
U = 1024
OFF = 8
ROUNDS = 2
step_size = 0.5


def move_down(products, tilt_table):
    base = jnp.zeros((products.shape[1] + OFF, U), jnp.float32)
    placed = jax.vmap(
        lambda block, shift_rows: lax.dynamic_update_slice(base, block, (shift_rows, jnp.int32(0)))
    )(products, tilt_table)
    return jnp.sum(placed, axis=0)


def backproject(extended, tilt_table, ray_weights, band_rows):
    slices_count = tilt_table.shape[1]
    running = jnp.zeros((slices_count * band_rows, X), jnp.float32)
    for angle_index in range(ray_weights.shape[0]):
        source = extended[angle_index]
        picked = jax.vmap(
            lambda shift_rows: lax.dynamic_slice(source, (shift_rows, jnp.int32(0)), (band_rows, U))
        )(tilt_table[angle_index])
        running = running + lax.dot_general(
            picked.reshape(slices_count * band_rows, U),
            ray_weights[angle_index],
            (((1,), (1,)), ((), ())),
            preferred_element_type=jnp.float32,
        )
    return running


def apply_update(current, running):
    partial_value = lax.optimization_barrier(running.reshape(current.shape).astype(jnp.bfloat16))
    partial_wide = partial_value.astype(jnp.float32)
    gradient = lax.psum(partial_wide, "ang")
    renewed = (current.astype(jnp.float32) - step_size * gradient).astype(jnp.bfloat16)
    return renewed


def per_device(volume, ray_weights, row_offsets, measured, shifts):
    angles_here = ray_weights.shape[0]
    band_rows = measured.shape[1]
    highest = lax.Precision.HIGHEST
    numbers = lax.iota(jnp.int32, U)
    turns = numbers[:, None] * numbers[None, :] % U
    radians = turns.astype(jnp.float32) * (2.0 * math.pi / U)
    cosine = jnp.cos(radians)
    sine = jnp.sin(radians)
    signed = jnp.where(numbers <= (U - 1) // 2, numbers, numbers - U)
    omega = signed.astype(jnp.float32) * (2.0 * math.pi / U)
    flat_rows = measured.reshape(angles_here * band_rows, U)
    real_part = jnp.dot(flat_rows, cosine, precision=highest).reshape(angles_here, band_rows, U)
    imag_part = -jnp.dot(flat_rows, sine, precision=highest).reshape(angles_here, band_rows, U)
    phase = omega[None, None, :] * shifts[:, None, None]
    turned_real = real_part * jnp.cos(phase) + imag_part * jnp.sin(phase)
    turned_imag = imag_part * jnp.cos(phase) - real_part * jnp.sin(phase)
    first_half = jnp.concatenate([turned_real, omega * turned_imag], axis=0).reshape(-1, U)
    second_half = jnp.concatenate([turned_imag, -omega * turned_real], axis=0).reshape(-1, U)
    inverse = (
        jnp.dot(first_half, cosine, precision=highest)
        - jnp.dot(second_half, sine, precision=highest)
    ) / U
    inverse = inverse.reshape(2, angles_here, band_rows, U)
    shifted = inverse[0]
    slope_field = inverse[1]
    projection = shifted
    residual = shifted
    current = volume
    slices_here = volume.shape[0]
    tilt_table = lax.dynamic_slice_in_dim(
        row_offsets, lax.axis_index("slab") * slices_here, slices_here, 1
    )
    for round_index in range(ROUNDS):
        flattened = current.reshape(slices_here * Y, X)
        partials = jnp.stack(
            [
                move_down(
                    jnp.dot(
                        flattened, ray_weights[angle_index], preferred_element_type=jnp.float32
                    ).reshape(slices_here, Y, U),
                    tilt_table[angle_index],
                )[:Y]
                for angle_index in range(angles_here)
            ]
        )
        projection = lax.psum_scatter(partials, "slab", scatter_dimension=1, tiled=True)
        residual = projection - shifted
        rounded = residual.astype(jnp.bfloat16)
        gathered = lax.all_gather(rounded, "slab", axis=1, tiled=True)
        extended = jnp.concatenate(
            [gathered, jnp.zeros((angles_here, OFF, U), jnp.bfloat16)], axis=1
        )
        running = backproject(extended, tilt_table, ray_weights, Y)
        current = apply_update(current, running)
    local_dot = jnp.sum(projection * slope_field, axis=(1, 2))
    shift_slope = lax.psum(local_dot, "slab") / math.sqrt(Y * U)
    return (current, residual, shift_slope)


def solution(mesh):
    in_specs = (
        P(("grp", "slab"), None, None),
        P("ang", None, None),
        P("ang", None),
        P(("grp", "ang"), "slab", None),
        P(("grp", "ang")),
    )
    out_specs = (P(("grp", "slab"), None, None), P(("grp", "ang"), "slab", None), P(("grp", "ang")))
    return jax.shard_map(
        per_device, mesh=mesh, in_specs=in_specs, out_specs=out_specs, check_vma=False
    )
```

profile of v0, /device:TPU:1, one launch (start us, length us, event | category | flops | bytes accessed | tf_op | source)
XLA Modules:
  0.0 434.2 jit_solution(13662559025870306911)
XLA Ops:
  7.3 4.6 %fusion.16 = f32[2,256,1024]{2,1,0:T(8,128)} fusion(bf16[2,256,1024]{2,1,0:T(8,128)(2,1)} %param.5, bf16[2,1024,1024]{2,1,0:T(8,128)(2,1)} %param.6), kind=kOutput, calls=%fused_computation.41 | convolution fusion | flops 1073741824 | bytes 5242880 | tf_op jit(solution)/shard_map/dot_general | solution.py:86
  11.9 2.6 fusion.8
  14.8 1.6 broadcast.119.clone.2
  16.4 23.4 %while.12 = (s32[]{:T(128)}, f32[2,264,1024]{2,1,0:T(8,128)}, s32[2,3]{1,0:T(2,128)S(1)}, f32[2,256,1024]{2,1,0:T(8,128)}, s32[]{:T(128)}, /*index=5*/s32[3]{0:T(128)S(1)}, s32[]{:T(128)}) while((s32[]{:T(128)}, f32[2,264,1024]{2,1,0:T(8,128)}, s32[2,3]{1,0:T(2,128)S(1)}, f32[2,256,1024]{2,1,0:T(8,128)}, s32[]{:T(128)}, /*index=5*/s32[3]{0:T(128)S(1)}, ...), condition=%wide.while_cond.4, body=%wide.while_body.4.sunk | while | flops 262163 | bytes 5243051 | solution.py:18
  17.0 2.6 and_reduce_fusion.8
  19.6 3.6 dynamic-slice_select_fusion.8
  23.2 4.9 %dynamic-update-slice.32 = f32[2,264,1024]{2,1,0:T(8,128)} dynamic-update-slice(f32[2,264,1024]{2,1,0:T(8,128)} %get-tuple-element.455, f32[1,256,1024]{2,1,0:T(8,128)S(1)} %dynamic-slice_select_fusion.8, s32[]{:T(128)} %bitcast.154, s32[]{:T(128)} %bitcast.155, s32[]{:T(128)} %constant.18.clone.1..sunk) | dynamic-update-slice | bytes 2097156 | tf_op jit(solution)/shard_map/vmap(vmap())/scatter
  28.7 2.6 and_reduce_fusion.8
  31.3 3.6 dynamic-slice_select_fusion.8
  34.9 4.9 %dynamic-update-slice.32 = f32[2,264,1024]{2,1,0:T(8,128)} dynamic-update-slice(f32[2,264,1024]{2,1,0:T(8,128)} %get-tuple-element.455, f32[1,256,1024]{2,1,0:T(8,128)S(1)} %dynamic-slice_select_fusion.8, s32[]{:T(128)} %bitcast.154, s32[]{:T(128)} %bitcast.155, s32[]{:T(128)} %constant.18.clone.1..sunk) | dynamic-update-slice | bytes 2097156 | tf_op jit(solution)/shard_map/vmap(vmap())/scatter
  39.9 1.6 broadcast.119.clone.1
  41.5 23.9 %while.13 = (s32[]{:T(128)}, f32[2,264,1024]{2,1,0:T(8,128)}, s32[2,3]{1,0:T(2,128)S(1)}, f32[2,256,1024]{2,1,0:T(8,128)}, s32[]{:T(128)}, /*index=5*/s32[3]{0:T(128)S(1)}, s32[]{:T(128)}) while((s32[]{:T(128)}, f32[2,264,1024]{2,1,0:T(8,128)}, s32[2,3]{1,0:T(2,128)S(1)}, f32[2,256,1024]{2,1,0:T(8,128)}, s32[]{:T(128)}, /*index=5*/s32[3]{0:T(128)S(1)}, ...), condition=%wide.while_cond.5, body=%wide.while_body.5.sunk | while | flops 262163 | bytes 5243051 | solution.py:18
  42.2 2.7 and_reduce_fusion.9
  44.9 3.7 dynamic-slice_select_fusion.9
  48.6 5.0 %dynamic-update-slice.33 = f32[2,264,1024]{2,1,0:T(8,128)} dynamic-update-slice(f32[2,264,1024]{2,1,0:T(8,128)} %get-tuple-element.434, f32[1,256,1024]{2,1,0:T(8,128)S(1)} %dynamic-slice_select_fusion.9, s32[]{:T(128)} %bitcast.159, s32[]{:T(128)} %bitcast.160, s32[]{:T(128)} %constant.18.clone.1..sunk.1) | dynamic-update-slice | bytes 2097156 | tf_op jit(solution)/shard_map/vmap(vmap())/scatter
  54.3 2.7 and_reduce_fusion.9
  57.0 3.7 dynamic-slice_select_fusion.9
  60.7 4.8 %dynamic-update-slice.33 = f32[2,264,1024]{2,1,0:T(8,128)} dynamic-update-slice(f32[2,264,1024]{2,1,0:T(8,128)} %get-tuple-element.434, f32[1,256,1024]{2,1,0:T(8,128)S(1)} %dynamic-slice_select_fusion.9, s32[]{:T(128)} %bitcast.159, s32[]{:T(128)} %bitcast.160, s32[]{:T(128)} %constant.18.clone.1..sunk.1) | dynamic-update-slice | bytes 2097156 | tf_op jit(solution)/shard_map/vmap(vmap())/scatter
  65.4 3.0 reduce_sum.45
  68.4 1.2 reduce_sum.46
  69.7 1.7 slice_bitcast_fusion.2
  71.4 1.5 pad_maximum_fusion
  73.6 18.6 %fusion.26 = f32[1024,128]{0,1:T(8,128)S(1)} fusion(f32[128,1024]{1,0:T(8,128)S(1)} %bitcast.174), kind=kOutput, calls=%fused_computation.54 | convolution fusion | flops 1625292800 | bytes 1048576 | tf_op jit(solution)/shard_map/dot_general | solution.py:60
  92.2 18.7 %fusion.50 = f32[1024,128]{0,1:T(8,128)S(1)} fusion(f32[128,1024]{1,0:T(8,128)S(1)} %bitcast.175), kind=kOutput, calls=%fused_computation.67 | convolution fusion | flops 1625423872 | bytes 1048576 | tf_op jit(solution)/shard_map/dot_general | solution.py:61
  111.3 20.2 %fusion.24 = f32[256,1024]{1,0:T(8,128)S(1)} fusion(f32[256,1024]{1,0:T(8,128)S(1)} %bitcast.185), kind=kOutput, calls=%fused_computation.53 | convolution fusion | flops 3235905536 | bytes 2097152 | tf_op jit(solution)/shard_map/dot_general | solution.py:68
  131.5 20.1 %fusion.47 = f32[256,1024]{1,0:T(8,128)S(1)} fusion(f32[256,1024]{1,0:T(8,128)S(1)} %fusion.24, f32[256,1024]{1,0:T(8,128)S(1)} %bitcast.184), kind=kOutput, calls=%fused_computation.66 | convolution fusion | flops 3236429824 | bytes 3145728 | tf_op jit(solution)/shard_map/dot_general | solution.py:69
  151.7 1.8 subtract_convert_fusion.2
  153.8 29.5 %all-gather.3.cloned.1.call-done = bf16[2,256,1024]{2,1,0:T(8,128)(2,1)} async-done(((bf16[2,64,1024]{2,1,0:T(8,128)(2,1)}), bf16[2,256,1024]{2,1,0:T(8,128)(2,1)}) %all-gather.3.cloned.1.call-update) | async-done | bytes 1048592 | tf_op jit(solution)/shard_map/all_gather | solution.py:97
  183.3 1.3 fusion.53
  185.3 4.2 fusion.10
  190.1 4.5 %add_convert_fusion.1 = bf16[512,1024]{1,0:T(8,128)(2,1)} fusion(f32[512,1024]{1,0:T(8,128)} %fusion.10, bf16[512,1024]{1,0:T(8,128)(2,1)S(1)} %bitcast.182, bf16[2,1024,1024]{2,1,0:T(8,128)(2,1)} %param.6), kind=kOutput, calls=%fused_computation.50 | convolution fusion | flops 1074790400 | bytes 6291456 | tf_op jit(solution)/shard_map/dot_general | solution.py:31
  194.6 42.1 %all-reduce.6 = f32[2,256,1024]{2,1,0:T(8,128)S(1)} all-reduce(bf16[2,256,1024]{2,1,0:T(8,128)(2,1)} %bitcast.178), channel_id=1, replica_groups=mesh['grp'=2,'slab'=4,'ang'=4] {'ang'}, use_global_device_ids=true, to_apply=%region_5.6 | all-reduce | flops 524288 | bytes 3145728 | tf_op jit(solution)/shard_map/psum | solution.py:43
  236.6 1.7 subtract_convert_fusion.1
  238.4 0.8 copy-done.10
  239.1 2.6 fusion.14
  241.7 2.6 fusion.6
  244.3 1.6 broadcast.119.clone.3
  245.9 23.4 %while.14 = (s32[]{:T(128)}, f32[2,264,1024]{2,1,0:T(8,128)}, s32[2,3]{1,0:T(2,128)S(1)}, f32[2,256,1024]{2,1,0:T(8,128)}, s32[]{:T(128)}, /*index=5*/s32[3]{0:T(128)S(1)}, s32[]{:T(128)}) while((s32[]{:T(128)}, f32[2,264,1024]{2,1,0:T(8,128)}, s32[2,3]{1,0:T(2,128)S(1)}, f32[2,256,1024]{2,1,0:T(8,128)}, s32[]{:T(128)}, /*index=5*/s32[3]{0:T(128)S(1)}, ...), condition=%wide.while_cond.6, body=%wide.while_body.6.sunk | while | flops 262163 | bytes 5243051 | solution.py:18
  246.5 2.6 and_reduce_fusion.10
  249.1 3.5 dynamic-slice_select_fusion.10
  252.7 5.0 %dynamic-update-slice.34 = f32[2,264,1024]{2,1,0:T(8,128)} dynamic-update-slice(f32[2,264,1024]{2,1,0:T(8,128)} %get-tuple-element.527, f32[1,256,1024]{2,1,0:T(8,128)S(1)} %dynamic-slice_select_fusion.10, s32[]{:T(128)} %bitcast.164, s32[]{:T(128)} %bitcast.165, s32[]{:T(128)} %constant.18.clone.1..sunk.2) | dynamic-update-slice | bytes 2097156 | tf_op jit(solution)/shard_map/vmap(vmap())/scatter
  258.3 2.6 and_reduce_fusion.10
  260.9 3.5 dynamic-slice_select_fusion.10
  264.4 5.0 %dynamic-update-slice.34 = f32[2,264,1024]{2,1,0:T(8,128)} dynamic-update-slice(f32[2,264,1024]{2,1,0:T(8,128)} %get-tuple-element.527, f32[1,256,1024]{2,1,0:T(8,128)S(1)} %dynamic-slice_select_fusion.10, s32[]{:T(128)} %bitcast.164, s32[]{:T(128)} %bitcast.165, s32[]{:T(128)} %constant.18.clone.1..sunk.2) | dynamic-update-slice | bytes 2097156 | tf_op jit(solution)/shard_map/vmap(vmap())/scatter
  269.4 1.9 reduce_sum.47
  271.4 1.6 broadcast.119.clone
  273.0 23.3 %while.15 = (s32[]{:T(128)}, f32[2,264,1024]{2,1,0:T(8,128)}, s32[2,3]{1,0:T(2,128)S(1)}, f32[2,256,1024]{2,1,0:T(8,128)}, s32[]{:T(128)}, /*index=5*/s32[3]{0:T(128)S(1)}, s32[]{:T(128)}) while((s32[]{:T(128)}, f32[2,264,1024]{2,1,0:T(8,128)}, s32[2,3]{1,0:T(2,128)S(1)}, f32[2,256,1024]{2,1,0:T(8,128)}, s32[]{:T(128)}, /*index=5*/s32[3]{0:T(128)S(1)}, ...), condition=%wide.while_cond.7, body=%wide.while_body.7.sunk | while | flops 262163 | bytes 5243051 | solution.py:18
  273.6 2.6 and_reduce_fusion.11
  276.2 3.6 dynamic-slice_select_fusion.11
  279.8 5.0 %dynamic-update-slice.35 = f32[2,264,1024]{2,1,0:T(8,128)} dynamic-update-slice(f32[2,264,1024]{2,1,0:T(8,128)} %get-tuple-element.506, f32[1,256,1024]{2,1,0:T(8,128)S(1)} %dynamic-slice_select_fusion.11, s32[]{:T(128)} %bitcast.169, s32[]{:T(128)} %bitcast.170, s32[]{:T(128)} %constant.18.clone.1..sunk.3) | dynamic-update-slice | bytes 2097156 | tf_op jit(solution)/shard_map/vmap(vmap())/scatter
  285.4 2.6 and_reduce_fusion.11
  288.0 3.5 dynamic-slice_select_fusion.11
  291.5 4.7 %dynamic-update-slice.35 = f32[2,264,1024]{2,1,0:T(8,128)} dynamic-update-slice(f32[2,264,1024]{2,1,0:T(8,128)} %get-tuple-element.506, f32[1,256,1024]{2,1,0:T(8,128)S(1)} %dynamic-slice_select_fusion.11, s32[]{:T(128)} %bitcast.169, s32[]{:T(128)} %bitcast.170, s32[]{:T(128)} %constant.18.clone.1..sunk.3) | dynamic-update-slice | bytes 2097156 | tf_op jit(solution)/shard_map/vmap(vmap())/scatter
  296.3 1.9 reduce_sum.48
  298.3 1.5 pad_maximum_fusion.1
  299.9 42.4 %reduce-scatter.5.cloned.1.call-done = f32[2,64,1024]{2,1,0:T(8,128)} async-done(((f32[2,256,1024]{2,1,0:T(8,128)}), f32[2,64,1024]{2,1,0:T(8,128)}) %reduce-scatter.5.cloned.1.call-update) | async-done | bytes 524304 | tf_op jit(solution)/shard_map/reduce_scatter | solution.py:94
  342.3 2.1 fusion.76
  344.4 8.7 %psum.23 = f32[2]{0:T(128)S(1)} all-reduce(f32[2]{0:T(128)S(1)} %get-tuple-element.189), channel_id=1, replica_groups=mesh['grp'=2,'slab'=4,'ang'=4] {'slab'}, use_global_device_ids=true, to_apply=%region_13.14 | all-reduce | flops 2 | bytes 16 | tf_op jit(solution)/shard_map/psum | solution.py:104
  353.6 18.1 %all-gather.5.cloned.1.call-done = bf16[2,256,1024]{2,1,0:T(8,128)(2,1)} async-done(((bf16[2,64,1024]{2,1,0:T(8,128)(2,1)}), bf16[2,256,1024]{2,1,0:T(8,128)(2,1)}) %all-gather.5.cloned.1.call-update) | async-done | bytes 1048592 | tf_op jit(solution)/shard_map/all_gather | solution.py:97
  371.6 1.3 fusion.55
  373.5 4.2 fusion.12
  378.2 4.5 %add_convert_fusion = bf16[512,1024]{1,0:T(8,128)(2,1)} fusion(f32[512,1024]{1,0:T(8,128)} %fusion.12, bf16[512,1024]{1,0:T(8,128)(2,1)S(1)} %bitcast.180, bf16[2,1024,1024]{2,1,0:T(8,128)(2,1)} %param.6), kind=kOutput, calls=%fused_computation.48 | convolution fusion | flops 1074790400 | bytes 6291456 | tf_op jit(solution)/shard_map/dot_general | solution.py:31
  382.7 42.2 %all-reduce.7 = f32[2,256,1024]{2,1,0:T(8,128)S(1)} all-reduce(bf16[2,256,1024]{2,1,0:T(8,128)(2,1)} %bitcast.179), channel_id=1, replica_groups=mesh['grp'=2,'slab'=4,'ang'=4] {'ang'}, use_global_device_ids=true, to_apply=%region_11.12 | all-reduce | flops 524288 | bytes 3145728 | tf_op jit(solution)/shard_map/psum | solution.py:43
  424.9 2.6 subtract_convert_fusion
  (90 shorter events, 11.5 us)
Async XLA Ops:
  7.2 66.5 %copy-start = (f32[2,64,1024]{2,1,0:T(8,128)S(1)}, f32[2,64,1024]{2,1,0:T(8,128)}, u32[]{:S(2)}) copy-start(f32[2,64,1024]{2,1,0:T(8,128)} %param.8) | copy-start | bytes 1572868
  7.2 144.5 %reduce-scatter.3.cloned.1.call-start = ((), (), s32[]{:S(2)}) async-start(), calls=%async_computation.2 | async-start | bytes 2621440 | tf_op jit(solution)/shard_map/reduce_scatter | solution.py:94
  7.2 4.7 %copy-start.4 = (bf16[2,256,1024]{2,1,0:T(8,128)(2,1)S(1)}, bf16[2,256,1024]{2,1,0:T(8,128)(2,1)}, u32[]{:S(2)}) copy-start(bf16[2,256,1024]{2,1,0:T(8,128)(2,1)} %param.5) | copy-start | bytes 3145732
  7.2 4.7 %copy-start.9 = (bf16[2,1024,1024]{2,1,0:T(8,128)(2,1)S(1)}, bf16[2,1024,1024]{2,1,0:T(8,128)(2,1)}, u32[]{:S(2)}) copy-start(bf16[2,1024,1024]{2,1,0:T(8,128)(2,1)} %param.6) | copy-start | bytes 12582916
  11.9 2.6 copy-start.6
  11.9 2.7 copy-start.7
  14.5 1.9 copy-start.5
  65.4 3.0 copy-start.2
  71.4 2.0 copy-start.8
  72.9 110.4 %all-gather.3.cloned.1.call-start = ((), (), s32[]{:S(2)}) async-start(), calls=%async_computation.3 | async-start | bytes 1310720 | tf_op jit(solution)/shard_map/all_gather | solution.py:97
  153.6 188.7 %reduce-scatter.5.cloned.1.call-start = ((), (), s32[]{:S(2)}) async-start(), calls=%async_computation.4 | async-start | bytes 2621440 | tf_op jit(solution)/shard_map/reduce_scatter | solution.py:94
  236.6 2.5 copy-start.10
  239.1 2.6 copy-start.3
  299.8 71.8 %all-gather.5.cloned.1.call-start = ((), (), s32[]{:S(2)}) async-start(), calls=%async_computation.5 | async-start | bytes 1310720 | tf_op jit(solution)/shard_map/all_gather | solution.py:97
  382.7 44.7 %copy-start.1 = (f32[2,64,1024]{2,1,0:T(8,128)S(1)}, f32[2,64,1024]{2,1,0:T(8,128)}, u32[]{:S(2)}) copy-start(f32[2,64,1024]{2,1,0:T(8,128)} %param.8) | copy-start | bytes 1572868
Sparse Core Ops, SparseCore 0:
  73.0 45.3 reduce-scatter.2
  153.7 29.5 all-gather.2
  299.9 42.2 reduce-scatter.4
  344.5 27.0 all-gather.4
where the time goes:
time: 440 us; the launch traced here: 434 us
  matrix products  107 us (24%)
  blocking collectives  92.9 us (21%)
  waiting for transfers between devices  90 us (20%)
  other arithmetic  70.2 us (16%)
  local copies, waits for them, and re-layouts  58.4 us (13%)
  between operations  14.3 us (3%)
    psum x2, blocking collectives, apply_update(): gradient = lax.psum(partial_wide, 'ang')  84.2 us
    scatter x16, other arithmetic  49.8 us
    all_gather x2, waiting for transfers between devices, per_device(): gathered = lax.all_gather(rounded, 'slab', axis=1, tiled=True)  47.5 us
    scatter x24, local copies, waits for them, and re-layouts  44.2 us
    reduce_scatter x2, waiting for transfers between devices, per_device(): lax.psum_scatter(partials, 'slab', scatter_dimension=1, tiled=True)  42.4 us
    dot_general x1, matrix products, per_device(): jnp.dot(first_half, cosine, precision=highest)  20.2 us
    dot_general x1, matrix products, per_device(): jnp.dot(second_half, sine, precision=highest)  20.1 us
    dot_general x1, matrix products, per_device(): jnp.dot(flat_rows, sine, precision=highest)  18.7 us
  transfers between devices with their start and end apart: 4, of which 3 were waited for; matrix products, arithmetic and copies ran while one was open for 18% of the time, Pallas kernels for 0%

commit v1 on v0

--- a/solution.py
+++ b/solution.py
@@ -40,7 +40,17 @@
 def apply_update(current, running):
     partial_value = lax.optimization_barrier(running.reshape(current.shape).astype(jnp.bfloat16))
     partial_wide = partial_value.astype(jnp.float32)
-    gradient = lax.psum(partial_wide, "ang")
+
+    def try_all_works(work_x):
+        size_here = lax.axis_size("ang")
+        low, front = (work_x, 0)
+        while 1 << front < size_here:
+            reply = lax.ppermute(low, "ang", [(jj, jj ^ 1 << front) for jj in range(size_here)])
+            low = low + reply
+            front = front + 1
+        return low
+
+    gradient = try_all_works(partial_wide)
     renewed = (current.astype(jnp.float32) - step_size * gradient).astype(jnp.bfloat16)
     return renewed
 

time: 440 us -> 463 us (1.052)
  waiting for transfers between devices: 90 us -> 191 us
  blocking collectives: 92.9 us -> 8.1 us
  starting transfers between devices: 0.63 us -> 5.56 us
    ppermute x0 -> x4, waiting for transfers between devices: none -> 90.4 us  [try_all_works(): lax.ppermute(low, 'ang', [(jj, jj ^ 1 << front) for jj in range(size_here)])]
    psum x2 -> x0, blocking collectives: 84.2 us -> none  [apply_update(): gradient = lax.psum(partial_wide, 'ang')]
    all_gather x2, waiting for transfers between devices: 47.5 us -> 56.7 us  [per_device(): gathered = lax.all_gather(rounded, 'slab', axis=1, tiled=True)]
    ppermute x0 -> x4, starting transfers between devices: none -> 4.93 us  [try_all_works(): lax.ppermute(low, 'ang', [(jj, jj ^ 1 << front) for jj in range(size_here)])]
  transfers between devices with their start and end apart: 4 -> 8, of which waited for: 3 -> 7; matrix products, arithmetic and copies ran while one was open for 18% -> 17% of each run, Pallas kernels for 0% -> 0%
where the time goes in v1:
time: 463 us; the launch traced here: 456 us
  waiting for transfers between devices  191 us (41%)
  matrix products  105 us (23%)
  other arithmetic  73.7 us (16%)
  local copies, waits for them, and re-layouts  57.9 us (13%)
  between operations  14.3 us (3%)
  blocking collectives  8.1 us (2%)
  starting transfers between devices  5.56 us (1%)
    ppermute x4, waiting for transfers between devices, try_all_works(): lax.ppermute(low, 'ang', [(jj, jj ^ 1 << front) for jj in range(size_here)])  90.4 us
    all_gather x2, waiting for transfers between devices, per_device(): gathered = lax.all_gather(rounded, 'slab', axis=1, tiled=True)  56.7 us
    scatter x16, other arithmetic  50.4 us
    scatter x24, local copies, waits for them, and re-layouts  44.4 us
    reduce_scatter x2, waiting for transfers between devices, per_device(): lax.psum_scatter(partials, 'slab', scatter_dimension=1, tiled=True)  43.6 us
    dot_general x1, matrix products, per_device(): jnp.dot(first_half, cosine, precision=highest)  20.2 us
    dot_general x1, matrix products, per_device(): jnp.dot(second_half, sine, precision=highest)  20.1 us
    dot_general x1, matrix products, per_device(): jnp.dot(flat_rows, sine, precision=highest)  18.7 us
  transfers between devices with their start and end apart: 8, of which 7 were waited for; matrix products, arithmetic and copies ran while one was open for 17% of the time, Pallas kernels for 0%

profile of v1, /device:TPU:1, one launch (start us, length us, event | category | flops | bytes accessed | tf_op | source)
XLA Modules:
  0.0 456.2 jit_solution(10557271269738979472)
XLA Ops:
  7.3 4.6 %fusion.16 = f32[2,256,1024]{2,1,0:T(8,128)} fusion(bf16[2,256,1024]{2,1,0:T(8,128)(2,1)} %param.5, bf16[2,1024,1024]{2,1,0:T(8,128)(2,1)} %param.6), kind=kOutput, calls=%fused_computation.41 | convolution fusion | flops 1073741824 | bytes 5242880 | tf_op jit(solution)/shard_map/dot_general | solution.py:96
  11.9 2.6 fusion.8
  14.8 1.6 broadcast.119.clone.2
  16.4 23.3 %while.12 = (s32[]{:T(128)}, f32[2,264,1024]{2,1,0:T(8,128)}, s32[2,3]{1,0:T(2,128)S(1)}, f32[2,256,1024]{2,1,0:T(8,128)}, s32[]{:T(128)}, /*index=5*/s32[3]{0:T(128)S(1)}, s32[]{:T(128)}) while((s32[]{:T(128)}, f32[2,264,1024]{2,1,0:T(8,128)}, s32[2,3]{1,0:T(2,128)S(1)}, f32[2,256,1024]{2,1,0:T(8,128)}, s32[]{:T(128)}, /*index=5*/s32[3]{0:T(128)S(1)}, ...), condition=%wide.while_cond.4, body=%wide.while_body.4.sunk | while | flops 262163 | bytes 5243051 | solution.py:18
  17.0 2.6 and_reduce_fusion.8
  19.6 3.6 dynamic-slice_select_fusion.8
  23.2 4.9 %dynamic-update-slice.32 = f32[2,264,1024]{2,1,0:T(8,128)} dynamic-update-slice(f32[2,264,1024]{2,1,0:T(8,128)} %get-tuple-element.455, f32[1,256,1024]{2,1,0:T(8,128)S(1)} %dynamic-slice_select_fusion.8, s32[]{:T(128)} %bitcast.154, s32[]{:T(128)} %bitcast.155, s32[]{:T(128)} %constant.18.clone.1..sunk) | dynamic-update-slice | bytes 2097156 | tf_op jit(solution)/shard_map/vmap(vmap())/scatter
  28.7 2.6 and_reduce_fusion.8
  31.3 3.6 dynamic-slice_select_fusion.8
  34.8 4.9 %dynamic-update-slice.32 = f32[2,264,1024]{2,1,0:T(8,128)} dynamic-update-slice(f32[2,264,1024]{2,1,0:T(8,128)} %get-tuple-element.455, f32[1,256,1024]{2,1,0:T(8,128)S(1)} %dynamic-slice_select_fusion.8, s32[]{:T(128)} %bitcast.154, s32[]{:T(128)} %bitcast.155, s32[]{:T(128)} %constant.18.clone.1..sunk) | dynamic-update-slice | bytes 2097156 | tf_op jit(solution)/shard_map/vmap(vmap())/scatter
  39.8 1.6 broadcast.119.clone.1
  41.4 24.2 %while.13 = (s32[]{:T(128)}, f32[2,264,1024]{2,1,0:T(8,128)}, s32[2,3]{1,0:T(2,128)S(1)}, f32[2,256,1024]{2,1,0:T(8,128)}, s32[]{:T(128)}, /*index=5*/s32[3]{0:T(128)S(1)}, s32[]{:T(128)}) while((s32[]{:T(128)}, f32[2,264,1024]{2,1,0:T(8,128)}, s32[2,3]{1,0:T(2,128)S(1)}, f32[2,256,1024]{2,1,0:T(8,128)}, s32[]{:T(128)}, /*index=5*/s32[3]{0:T(128)S(1)}, ...), condition=%wide.while_cond.5, body=%wide.while_body.5.sunk | while | flops 262163 | bytes 5243051 | solution.py:18
  42.1 2.7 and_reduce_fusion.9
  44.8 3.7 dynamic-slice_select_fusion.9
  48.6 5.1 %dynamic-update-slice.33 = f32[2,264,1024]{2,1,0:T(8,128)} dynamic-update-slice(f32[2,264,1024]{2,1,0:T(8,128)} %get-tuple-element.434, f32[1,256,1024]{2,1,0:T(8,128)S(1)} %dynamic-slice_select_fusion.9, s32[]{:T(128)} %bitcast.159, s32[]{:T(128)} %bitcast.160, s32[]{:T(128)} %constant.18.clone.1..sunk.1) | dynamic-update-slice | bytes 2097156 | tf_op jit(solution)/shard_map/vmap(vmap())/scatter
  54.3 2.7 and_reduce_fusion.9
  57.1 3.7 dynamic-slice_select_fusion.9
  60.8 4.8 %dynamic-update-slice.33 = f32[2,264,1024]{2,1,0:T(8,128)} dynamic-update-slice(f32[2,264,1024]{2,1,0:T(8,128)} %get-tuple-element.434, f32[1,256,1024]{2,1,0:T(8,128)S(1)} %dynamic-slice_select_fusion.9, s32[]{:T(128)} %bitcast.159, s32[]{:T(128)} %bitcast.160, s32[]{:T(128)} %constant.18.clone.1..sunk.1) | dynamic-update-slice | bytes 2097156 | tf_op jit(solution)/shard_map/vmap(vmap())/scatter
  65.6 3.0 reduce_sum.45
  69.9 1.7 slice_bitcast_fusion.2
  71.6 1.5 pad_maximum_fusion
  73.9 18.6 %fusion.26 = f32[1024,128]{0,1:T(8,128)S(1)} fusion(f32[128,1024]{1,0:T(8,128)S(1)} %bitcast.174), kind=kOutput, calls=%fused_computation.54 | convolution fusion | flops 1625292800 | bytes 1048576 | tf_op jit(solution)/shard_map/dot_general | solution.py:70
  92.5 18.7 %fusion.50 = f32[1024,128]{0,1:T(8,128)S(1)} fusion(f32[128,1024]{1,0:T(8,128)S(1)} %bitcast.175), kind=kOutput, calls=%fused_computation.67 | convolution fusion | flops 1625423872 | bytes 1048576 | tf_op jit(solution)/shard_map/dot_general | solution.py:71
  111.5 20.2 %fusion.24 = f32[256,1024]{1,0:T(8,128)S(1)} fusion(f32[256,1024]{1,0:T(8,128)S(1)} %bitcast.187), kind=kOutput, calls=%fused_computation.53 | convolution fusion | flops 3235905536 | bytes 2097152 | tf_op jit(solution)/shard_map/dot_general | solution.py:78
  131.7 20.1 %fusion.47 = f32[256,1024]{1,0:T(8,128)S(1)} fusion(f32[256,1024]{1,0:T(8,128)S(1)} %fusion.24, f32[256,1024]{1,0:T(8,128)S(1)} %bitcast.186), kind=kOutput, calls=%fused_computation.66 | convolution fusion | flops 3236429824 | bytes 3145728 | tf_op jit(solution)/shard_map/dot_general | solution.py:79
  152.0 1.8 subtract_convert_fusion.2
  154.0 29.4 %all-gather.3.cloned.1.call-done = bf16[2,256,1024]{2,1,0:T(8,128)(2,1)} async-done(((bf16[2,64,1024]{2,1,0:T(8,128)(2,1)}), bf16[2,256,1024]{2,1,0:T(8,128)(2,1)}) %all-gather.3.cloned.1.call-update) | async-done | bytes 1048592 | tf_op jit(solution)/shard_map/all_gather | solution.py:107
  183.5 1.3 fusion.53
  185.5 4.2 fusion.10
  190.3 3.5 add_convert_fusion.1
  195.3 3.8 collective-permute-done
  200.7 45.7 %collective-permute-done.1 = f32[2,256,1024]{2,1,0:T(8,128)} collective-permute-done((f32[2,256,1024]{2,1,0:T(8,128)S(1)}, f32[2,256,1024]{2,1,0:T(8,128)}, u32[]{:S(2)}, u32[]{:S(2)}) %collective-permute-start.1) | collective-permute-done | bytes 2097184 | tf_op jit(solution)/shard_map/ppermute | solution.py:48
  246.4 2.5 subtract_convert_fusion.1
  248.9 2.6 fusion.14
  251.5 2.6 fusion.6
  254.1 1.6 broadcast.119.clone.3
  255.7 23.7 %while.14 = (s32[]{:T(128)}, f32[2,264,1024]{2,1,0:T(8,128)}, s32[2,3]{1,0:T(2,128)S(1)}, f32[2,256,1024]{2,1,0:T(8,128)}, s32[]{:T(128)}, /*index=5*/s32[3]{0:T(128)S(1)}, s32[]{:T(128)}) while((s32[]{:T(128)}, f32[2,264,1024]{2,1,0:T(8,128)}, s32[2,3]{1,0:T(2,128)S(1)}, f32[2,256,1024]{2,1,0:T(8,128)}, s32[]{:T(128)}, /*index=5*/s32[3]{0:T(128)S(1)}, ...), condition=%wide.while_cond.6, body=%wide.while_body.6.sunk | while | flops 262163 | bytes 5243051 | solution.py:18
  256.3 2.6 and_reduce_fusion.10
  258.9 3.7 dynamic-slice_select_fusion.10
  262.6 5.0 %dynamic-update-slice.34 = f32[2,264,1024]{2,1,0:T(8,128)} dynamic-update-slice(f32[2,264,1024]{2,1,0:T(8,128)} %get-tuple-element.527, f32[1,256,1024]{2,1,0:T(8,128)S(1)} %dynamic-slice_select_fusion.10, s32[]{:T(128)} %bitcast.164, s32[]{:T(128)} %bitcast.165, s32[]{:T(128)} %constant.18.clone.1..sunk.2) | dynamic-update-slice | bytes 2097156 | tf_op jit(solution)/shard_map/vmap(vmap())/scatter
  268.2 2.6 and_reduce_fusion.10
  270.8 3.7 dynamic-slice_select_fusion.10
  274.5 5.0 %dynamic-update-slice.34 = f32[2,264,1024]{2,1,0:T(8,128)} dynamic-update-slice(f32[2,264,1024]{2,1,0:T(8,128)} %get-tuple-element.527, f32[1,256,1024]{2,1,0:T(8,128)S(1)} %dynamic-slice_select_fusion.10, s32[]{:T(128)} %bitcast.164, s32[]{:T(128)} %bitcast.165, s32[]{:T(128)} %constant.18.clone.1..sunk.2) | dynamic-update-slice | bytes 2097156 | tf_op jit(solution)/shard_map/vmap(vmap())/scatter
  279.5 1.9 reduce_sum.47
  281.5 1.6 broadcast.119.clone
  283.1 23.7 %while.15 = (s32[]{:T(128)}, f32[2,264,1024]{2,1,0:T(8,128)}, s32[2,3]{1,0:T(2,128)S(1)}, f32[2,256,1024]{2,1,0:T(8,128)}, s32[]{:T(128)}, /*index=5*/s32[3]{0:T(128)S(1)}, s32[]{:T(128)}) while((s32[]{:T(128)}, f32[2,264,1024]{2,1,0:T(8,128)}, s32[2,3]{1,0:T(2,128)S(1)}, f32[2,256,1024]{2,1,0:T(8,128)}, s32[]{:T(128)}, /*index=5*/s32[3]{0:T(128)S(1)}, ...), condition=%wide.while_cond.7, body=%wide.while_body.7.sunk | while | flops 262163 | bytes 5243051 | solution.py:18
  283.8 2.7 and_reduce_fusion.11
  286.4 3.7 dynamic-slice_select_fusion.11
  290.1 5.0 %dynamic-update-slice.35 = f32[2,264,1024]{2,1,0:T(8,128)} dynamic-update-slice(f32[2,264,1024]{2,1,0:T(8,128)} %get-tuple-element.506, f32[1,256,1024]{2,1,0:T(8,128)S(1)} %dynamic-slice_select_fusion.11, s32[]{:T(128)} %bitcast.169, s32[]{:T(128)} %bitcast.170, s32[]{:T(128)} %constant.18.clone.1..sunk.3) | dynamic-update-slice | bytes 2097156 | tf_op jit(solution)/shard_map/vmap(vmap())/scatter
  295.7 2.7 and_reduce_fusion.11
  298.4 3.7 dynamic-slice_select_fusion.11
  302.0 4.7 %dynamic-update-slice.35 = f32[2,264,1024]{2,1,0:T(8,128)} dynamic-update-slice(f32[2,264,1024]{2,1,0:T(8,128)} %get-tuple-element.506, f32[1,256,1024]{2,1,0:T(8,128)S(1)} %dynamic-slice_select_fusion.11, s32[]{:T(128)} %bitcast.169, s32[]{:T(128)} %bitcast.170, s32[]{:T(128)} %constant.18.clone.1..sunk.3) | dynamic-update-slice | bytes 2097156 | tf_op jit(solution)/shard_map/vmap(vmap())/scatter
  306.8 1.9 reduce_sum.48
  308.8 1.5 pad_maximum_fusion.1
  310.4 43.6 %reduce-scatter.5.cloned.1.call-done = f32[2,64,1024]{2,1,0:T(8,128)} async-done(((f32[2,256,1024]{2,1,0:T(8,128)}), f32[2,64,1024]{2,1,0:T(8,128)}) %reduce-scatter.5.cloned.1.call-update) | async-done | bytes 524304 | tf_op jit(solution)/shard_map/reduce_scatter | solution.py:104
  354.0 2.1 fusion.76
  356.1 27.2 %all-gather.5.cloned.1.call-done = bf16[2,256,1024]{2,1,0:T(8,128)(2,1)} async-done(((bf16[2,64,1024]{2,1,0:T(8,128)(2,1)}), bf16[2,256,1024]{2,1,0:T(8,128)(2,1)}) %all-gather.5.cloned.1.call-update) | async-done | bytes 1048592 | tf_op jit(solution)/shard_map/all_gather | solution.py:107
  383.3 1.3 fusion.55
  385.2 4.2 fusion.12
  390.0 3.5 add_convert_fusion
  394.9 3.8 collective-permute-done.2
  400.3 8.1 %psum.7 = f32[2]{0:T(128)S(1)} all-reduce(f32[2]{0:T(128)S(1)} %get-tuple-element.189), channel_id=1, replica_groups=mesh['grp'=2,'slab'=4,'ang'=4] {'slab'}, use_global_device_ids=true, to_apply=%region_11.12 | all-reduce | flops 2 | bytes 16 | tf_op jit(solution)/shard_map/psum | solution.py:114
  408.9 37.1 %collective-permute-done.3 = f32[2,256,1024]{2,1,0:T(8,128)} collective-permute-done((f32[2,256,1024]{2,1,0:T(8,128)S(1)}, f32[2,256,1024]{2,1,0:T(8,128)}, u32[]{:S(2)}, u32[]{:S(2)}) %collective-permute-start.3) | collective-permute-done | bytes 2097184 | tf_op jit(solution)/shard_map/ppermute | solution.py:48
  446.1 3.4 subtract_convert_fusion
  (100 shorter events, 19.0 us)
Async XLA Ops:
  7.2 66.7 %copy-start = (f32[2,64,1024]{2,1,0:T(8,128)S(1)}, f32[2,64,1024]{2,1,0:T(8,128)}, u32[]{:S(2)}) copy-start(f32[2,64,1024]{2,1,0:T(8,128)} %param.8) | copy-start | bytes 1572868
  7.2 144.8 %reduce-scatter.3.cloned.1.call-start = ((), (), s32[]{:S(2)}) async-start(), calls=%async_computation.2 | async-start | bytes 2621440 | tf_op jit(solution)/shard_map/reduce_scatter | solution.py:104
  7.2 4.7 %copy-start.4 = (bf16[2,256,1024]{2,1,0:T(8,128)(2,1)S(1)}, bf16[2,256,1024]{2,1,0:T(8,128)(2,1)}, u32[]{:S(2)}) copy-start(bf16[2,256,1024]{2,1,0:T(8,128)(2,1)} %param.5) | copy-start | bytes 3145732
  7.2 4.7 %copy-start.9 = (bf16[2,1024,1024]{2,1,0:T(8,128)(2,1)S(1)}, bf16[2,1024,1024]{2,1,0:T(8,128)(2,1)}, u32[]{:S(2)}) copy-start(bf16[2,1024,1024]{2,1,0:T(8,128)(2,1)} %param.6) | copy-start | bytes 12582916
  11.9 2.6 copy-start.6
  11.9 2.7 copy-start.7
  14.5 1.9 copy-start.5
  65.6 3.0 copy-start.2
  71.6 2.1 copy-start.8
  73.1 110.4 %all-gather.3.cloned.1.call-start = ((), (), s32[]{:S(2)}) async-start(), calls=%async_computation.3 | async-start | bytes 1310720 | tf_op jit(solution)/shard_map/all_gather | solution.py:107
  153.8 200.2 %reduce-scatter.5.cloned.1.call-start = ((), (), s32[]{:S(2)}) async-start(), calls=%async_computation.4 | async-start | bytes 2621440 | tf_op jit(solution)/shard_map/reduce_scatter | solution.py:104
  194.1 5.0 %collective-permute-start = (f32[2,256,1024]{2,1,0:T(8,128)S(1)}, f32[2,256,1024]{2,1,0:T(8,128)S(1)}, u32[]{:S(2)}, u32[]{:S(2)}) collective-permute-start(f32[2,256,1024]{2,1,0:T(8,128)S(1)} %convert_element_type.65), channel_id=1, source_target_pairs={{0,1},{1,0},{2,3},{3,2},{4,5},{5,4},{6,7},{7,6},{8,9},{9,8},{10,11... | collective-permute-start | bytes 6291464 | tf_op jit(solution)/shard_map/ppermute | solution.py:48
  199.4 47.0 %collective-permute-start.1 = (f32[2,256,1024]{2,1,0:T(8,128)S(1)}, f32[2,256,1024]{2,1,0:T(8,128)}, u32[]{:S(2)}, u32[]{:S(2)}) collective-permute-start(f32[2,256,1024]{2,1,0:T(8,128)S(1)} %convert_add_fusion.1), channel_id=1, source_target_pairs={{0,2},{1,3},{2,0},{3,1},{4,6},{5,7},{6,4},{7,5},{8,10},{9,11},{10,... | collective-permute-start | bytes 6291464 | tf_op jit(solution)/shard_map/ppermute | solution.py:48
  200.7 48.2 %copy-start.10 = (bf16[2,1024,1024]{2,1,0:T(8,128)(2,1)S(1)}, bf16[2,1024,1024]{2,1,0:T(8,128)(2,1)}, u32[]{:S(2)}) copy-start(bf16[2,1024,1024]{2,1,0:T(8,128)(2,1)} %param.6) | copy-start | bytes 12582916
  248.9 2.6 copy-start.3
  310.3 73.0 %all-gather.5.cloned.1.call-start = ((), (), s32[]{:S(2)}) async-start(), calls=%async_computation.5 | async-start | bytes 1310720 | tf_op jit(solution)/shard_map/all_gather | solution.py:107
  393.7 5.0 %collective-permute-start.2 = (f32[2,256,1024]{2,1,0:T(8,128)S(1)}, f32[2,256,1024]{2,1,0:T(8,128)S(1)}, u32[]{:S(2)}, u32[]{:S(2)}) collective-permute-start(f32[2,256,1024]{2,1,0:T(8,128)S(1)} %convert_element_type.71), channel_id=1, source_target_pairs={{0,1},{1,0},{2,3},{3,2},{4,5},{5,4},{6,7},{7,6},{8,9},{9,8},{10,11... | collective-permute-start | bytes 6291464 | tf_op jit(solution)/shard_map/ppermute | solution.py:48
  399.1 47.0 %collective-permute-start.3 = (f32[2,256,1024]{2,1,0:T(8,128)S(1)}, f32[2,256,1024]{2,1,0:T(8,128)}, u32[]{:S(2)}, u32[]{:S(2)}) collective-permute-start(f32[2,256,1024]{2,1,0:T(8,128)S(1)} %convert_add_fusion), channel_id=1, source_target_pairs={{0,2},{1,3},{2,0},{3,1},{4,6},{5,7},{6,4},{7,5},{8,10},{9,11},{10,... | collective-permute-start | bytes 6291464 | tf_op jit(solution)/shard_map/ppermute | solution.py:48
  408.4 41.1 %copy-start.1 = (f32[2,64,1024]{2,1,0:T(8,128)S(1)}, f32[2,64,1024]{2,1,0:T(8,128)}, u32[]{:S(2)}) copy-start(f32[2,64,1024]{2,1,0:T(8,128)} %param.8) | copy-start | bytes 1572868
Sparse Core Ops, SparseCore 0:
  73.2 45.2 reduce-scatter.2
  153.9 29.5 all-gather.2
  310.5 43.4 reduce-scatter.4
  356.2 27.0 all-gather.4
